TPU v7x, 32 devices: a whole 2x2x4 slice. The times are simulated.
32 devices in a mesh: clu: 16 (over z, x, core), doc: 2 (over y).
Axes of the slice: x: 2, y: 2, z: 4, core: 2. Of those that a mesh axis runs over, the one named last changes fastest.
Arguments:
- docs: bfloat16 [8192, 768], P(('clu', 'doc')), may hold values from -6 to 6
- centroids: bfloat16 [5504, 768], P('doc', 'clu'), may hold values from -6 to 6
- assigned: int32 [8192], P(('clu', 'doc')), may hold values from 0 to 5503
Outputs:
- nearest: float32 [8192], P(('clu', 'doc'))
- assigned_dist: float32 [8192], P(('clu', 'doc'))
Inputs may be any that keep to these rules, and one draw needn't show every extreme that they name: `assigned`: cluster ids.
All inputs are finite; a program needn't handle non-finite values.
Results may differ from a plain program's by a relative error of at most 0.0003.
Values may be sent and summed in bfloat16 or wider, within the bound.
A program may use at most 64 MiB of HBM per device.

v0:
```python
import jax
import jax.numpy as jnp
from jax import lax
from jax.sharding import PartitionSpec as P

epsilon = 1e-06


def merged(part, axis, combine):
    gathered = jax.tree.map(lambda a: lax.all_gather(a, axis), part)

    def take(source):
        return jax.tree.map(lambda a: lax.dynamic_index_in_dim(a, source, 0, False), gathered)

    return lax.fori_loop(
        1, lax.axis_size(axis), lambda source, state: combine(state, take(source)), take(0)
    )


def combine_pairs(first, second):
    return (jnp.minimum(first[0], second[0]), first[1] + second[1])


def row_scales(values):
    wide = values.astype(jnp.float32)
    return lax.rsqrt(jnp.sum(wide * wide, 1) + epsilon)


def distances(rows, cents):
    products = lax.dot_general(
        rows, cents, (((1,), (1,)), ((), ())), preferred_element_type=jnp.float32
    )
    return 1.0 - products * row_scales(rows)[:, None] * row_scales(cents)[None, :]


def on_device(docs, centroids, assigned):
    rows_dev = docs.shape[0]
    block = lax.all_gather(centroids, "clu", axis=1, tiled=True)
    group_rows, group_ids = (
        lax.all_gather(docs, "doc", axis=0, tiled=True),
        lax.all_gather(assigned, "doc", axis=0, tiled=True),
    )
    distance = distances(group_rows, block)
    block_count = block.shape[0]
    global_ids = lax.axis_index("doc") * block_count + jnp.arange(block_count, dtype=jnp.int32)
    matches = group_ids[:, None] == global_ids[None, :]
    chosen_part = jnp.sum(jnp.where(matches, distance, 0.0), 1)
    nearest_part = jnp.min(distance, 1)
    nearest_all, chosen_all = merged((nearest_part, chosen_part), "doc", combine_pairs)
    offset = lax.axis_index("doc") * rows_dev
    nearest = lax.dynamic_slice_in_dim(nearest_all, offset, rows_dev, 0)
    chosen = lax.dynamic_slice_in_dim(chosen_all, offset, rows_dev, 0)
    return (nearest, chosen)


def solution(mesh):
    placed = (P(("clu", "doc"), None), P("doc", "clu"), P(("clu", "doc")))
    return jax.shard_map(
        on_device,
        mesh=mesh,
        in_specs=placed,
        out_specs=(P(("clu", "doc")), P(("clu", "doc"))),
        check_vma=False,
    )
```

profile of v0, /device:TPU:0, one launch (start us, length us, event | category | flops | bytes accessed | tf_op | source)
XLA Modules:
  0.0 87.5 jit_solution(5234677581107313615)
XLA Ops:
  7.2 0.0 all-gather.7.cloned.1.call-start
  7.2 0.7 all-gather.7.cloned.1.call-update
  7.9 5.5 %all-gather.3 = s32[2,1,256]{2,1,0:T(1,128)S(1)} all-gather(s32[1,1,256]{2,1,0:T(1,128)} %bitcast.11), channel_id=1, replica_groups=mesh['clu'=16,'doc'=2] {'doc'}, dimensions={0}, use_global_device_ids=true | all-gather | bytes 3072 | tf_op jit(solution)/shard_map/all_gather | solution.py:41
  13.4 10.8 %all_gather.21 = bf16[512,768]{1,0:T(8,128)(2,1)S(1)} all-gather(bf16[256,768]{1,0:T(8,128)(2,1)} %param.3), channel_id=1, replica_groups=mesh['clu'=16,'doc'=2] {'doc'}, dimensions={0}, use_global_device_ids=true | all-gather | bytes 1179648 | tf_op jit(solution)/shard_map/all_gather | solution.py:40
  24.2 0.2 multiply_reduce_fusion.1
  24.5 39.6 %all-gather.7.cloned.1.call-done = bf16[2752,768]{0,1:T(8,128)(2,1)} async-done(((bf16[2752,48]{0,1:T(8,128)(2,1)}), bf16[2752,768]{0,1:T(8,128)(2,1)}) %all-gather.7.cloned.1.call-update) | async-done | bytes 4227088 | tf_op jit(solution)/shard_map/all_gather | solution.py:38
  64.1 0.0 copy-start
  64.1 3.3 %multiply_reduce_fusion = f32[2752]{0:T(1024)S(1)} fusion(bf16[2752,768]{0,1:T(8,128)(2,1)} %all-gather.7.cloned.1.call-done), kind=kLoop, calls=%fused_computation | loop fusion | flops 6337856 | bytes 4238080 | tf_op jit(solution)/shard_map/reduce_sum | solution.py:26
  67.4 0.2 copy-done
  67.6 3.7 %select_reduce_fusion = (f32[512]{0:T(512)S(1)}, f32[512]{0:T(512)S(1)}) fusion(s32[512]{0:T(512)S(1)} %bitcast.10, s32[2752]{0:T(1024)S(1)} %iota_add_fusion, f32[2752]{0:T(1024)S(1)} %add_rsqrt_fusion, f32[512]{0:T(512)S(1)} %add_rsqrt_fusion.1, bf16[512,768]{1,0:T(8,128)(2,1)S(1)} %all_gather.21, bf16[2752,768]{0,1:T(8,128)(2,1)S(1)} %copy-done), kind=kOutput, calls=%fused_computation.1 | convolution fusion | flops 2174123008 | bytes 5043712 | tf_op jit(solution)/shard_map/dot_general | solution.py:30
  71.3 4.4 %all-gather.2 = f32[2,1,512]{2,1,0:T(1,128)S(1)} all-gather(f32[1,1,512]{2,1,0:T(1,128)S(1)} %bitcast.9), channel_id=2, replica_groups=mesh['clu'=16,'doc'=2] {'doc'}, dimensions={0}, use_global_device_ids=true | all-gather | bytes 6144 | tf_op jit(solution)/shard_map/all_gather | solution.py:10
  75.7 4.4 %all-gather.4 = f32[2,1,512]{2,1,0:T(1,128)S(1)} all-gather(f32[1,1,512]{2,1,0:T(1,128)S(1)} %bitcast.8), channel_id=3, replica_groups=mesh['clu'=16,'doc'=2] {'doc'}, dimensions={0}, use_global_device_ids=true | all-gather | bytes 6144 | tf_op jit(solution)/shard_map/all_gather | solution.py:10
  80.1 0.6 dynamic-slice_add_fusion
  (5 shorter events, 0.0 us)
Async XLA Ops:
  7.2 56.9 %all-gather.7.cloned.1.call-start = ((), (), s32[]{:S(2)}) async-start(), calls=%async_computation | async-start | bytes 4595712 | tf_op jit(solution)/shard_map/all_gather | solution.py:38
  64.1 3.5 %copy-start = (bf16[2752,768]{0,1:T(8,128)(2,1)S(1)}, bf16[2752,768]{0,1:T(8,128)(2,1)}, u32[]{:S(2)}) copy-start(bf16[2752,768]{0,1:T(8,128)(2,1)} %all-gather.7.cloned.1.call-done) | copy-start | bytes 12681220
Sparse Core Ops, SparseCore 0:
  10.3 53.7 all-gather.6
where the time goes:
time: 87.7 us; the launch traced here: 87.5 us
  waiting for transfers between devices  40.3 us (46%)
  blocking collectives  25.1 us (29%)
  between operations  14 us (16%)
  other arithmetic  4.09 us (5%)
  matrix products  3.71 us (4%)
    all_gather x1, waiting for transfers between devices, on_device(): block = lax.all_gather(centroids, 'clu', axis=1, tiled=True)  39.6 us
    all_gather x1, blocking collectives, on_device(): lax.all_gather(docs, 'doc', axis=0, tiled=True)  10.8 us
    all_gather x2, blocking collectives, merged(): gathered = jax.tree.map(lambda a: lax.all_gather(a, axis), part)  8.72 us
    all_gather x1, blocking collectives, on_device(): lax.all_gather(assigned, 'doc', axis=0, tiled=True)  5.48 us
    dot_general x1, matrix products, distances(): lax.dot_general(rows, cents, (((1,), (1,)), ((), ())), preferred_element_...  3.71 us
    reduce_sum x2, other arithmetic, row_scales(): return lax.rsqrt(jnp.sum(wide * wide, 1) + epsilon)  3.5 us
  transfers between devices with their start and end apart: 1, of which 1 were waited for; matrix products, arithmetic and copies ran while one was open for 0% of the time, Pallas kernels for 0%

commit v1 on v0

v1 whole, which is shorter than its diff:
```python
import functools

import jax
import jax.numpy as jnp
from jax import lax
from jax.experimental import pallas as pl
from jax.experimental.pallas import tpu as pltpu
from jax.sharding import PartitionSpec as P

epsilon = 1e-06
TILE = 256
MESH = pl.DeviceIdType.MESH


def chip_at(pos, n):
    half = n // 2
    return jnp.where(pos < half, 2 * pos, 2 * (n - 1 - pos) + 1)


def kernel(n, nd, feat, docs_in, cents_in, ids_in, near_out, chosen_out,
           buf, docs_all, ids_all, dp_a, dp_b, dp_c, acc, idb, mx, ch, csq, scale, res, got,
           local_sem, ring_send, pair_send, recv, docs_send, docs_recv, ids_send, ids_recv,
           res_send, res_recv):
    hops = n // 2
    fp = cents_in.shape[0]
    width = cents_in.shape[1]
    rows_dev = docs_in.shape[0]
    cut = (width // 2 + 127) // 128 * 128
    chunks = ((0, cut), (cut, width - cut))

    clu, doc = lax.axis_index("clu"), lax.axis_index("doc")
    core, chip = lax.rem(clu, 2), lax.div(clu, 2)
    z, x = lax.div(chip, 2), lax.rem(chip, 2)
    pos = jnp.where(x == 0, z, n - 1 - z)
    right = chip_at(lax.rem(pos + 1, n), n) * 2 + core
    left = chip_at(lax.rem(pos + n - 1, n), n) * 2 + core
    partner = chip * 2 + (1 - core)

    own_c = pltpu.make_async_copy(cents_in, buf.at[pl.ds(0, fp), :], local_sem.at[0])
    own_d = pltpu.make_async_copy(docs_in, docs_all.at[0], local_sem.at[1])
    own_i = pltpu.make_async_copy(ids_in, ids_all.at[0], local_sem.at[2])
    own_c.start()
    own_d.start()
    own_i.start()

    barrier = pltpu.get_barrier_semaphore()
    for peer in (left, right, partner):
        pl.semaphore_signal(barrier, inc=1, device_id={"clu": peer}, device_id_type=MESH)
    for k in range(1, nd):
        pl.semaphore_signal(barrier, inc=1, device_id={"doc": lax.rem(doc + k, nd)}, device_id_type=MESH)
    pl.semaphore_wait(barrier, 3 + nd - 1)

    def slot(way, h):
        if h == 0:
            return 0
        if h == hops:
            return n - 1
        return 2 * h - 1 if way == 0 else 2 * h

    def piece(s, m, c):
        return buf.at[pl.ds((2 * s + m) * fp, fp), pl.ds(*chunks[c])]

    def reach(way, c):
        return hops if way == c else hops - 1

    sent = []

    def ring(way, h, c):
        s, t = slot(way, h), slot(way, h + 1)
        copy = pltpu.make_async_remote_copy(
            src_ref=piece(s, 0, c), dst_ref=piece(t, 0, c),
            send_sem=ring_send.at[way, h, c], recv_sem=recv.at[t, 0, c],
            device_id={"clu": right if way == 0 else left}, device_id_type=MESH)
        copy.start()
        sent.append(copy)

    def share(s, c):
        copy = pltpu.make_async_remote_copy(
            src_ref=piece(s, 0, c), dst_ref=piece(s, 1, c),
            send_sem=pair_send.at[s, c], recv_sem=recv.at[s, 1, c],
            device_id={"clu": partner}, device_id_type=MESH)
        copy.start()
        sent.append(copy)

    def landed(s, m, c):
        pltpu.make_async_remote_copy(
            src_ref=piece(s, m, c), dst_ref=piece(s, m, c),
            send_sem=pair_send.at[s, c], recv_sem=recv.at[s, m, c],
            device_id={"clu": partner}, device_id_type=MESH).wait_recv()

    own_c.wait()
    for way, c in ((0, 0), (1, 1), (0, 1), (1, 0)):
        ring(way, 0, c)
    for c in (0, 1):
        share(0, c)
    own_d.wait()
    own_i.wait()
    doc_copies = []
    for k in range(1, nd):
        mate = lax.rem(doc + k, nd)
        for ref, ss, rs in ((ids_all, ids_send, ids_recv), (docs_all, docs_send, docs_recv)):
            copy = pltpu.make_async_remote_copy(
                src_ref=ref.at[0], dst_ref=ref.at[k], send_sem=ss.at[k], recv_sem=rs.at[k],
                device_id={"doc": mate}, device_id_type=MESH)
            copy.start()
            doc_copies.append(copy)

    def owner(s):
        if s == 0:
            p = pos
        elif s == n - 1:
            p = pos + hops
        elif s % 2:
            p = pos + n - (s + 1) // 2
        else:
            p = pos + s // 2
        return chip_at(lax.rem(p, n), n)

    ranges = ((0, n - 3), (n - 3, n - 1), (n - 1, n))
    spread = (dp_a, dp_b, dp_c)

    def permute(k):
        rows = docs_all[k]
        for (first, last), out in zip(ranges, spread):
            wide = out.shape[1]
            lane = lax.broadcasted_iota(jnp.int32, (1, wide), 1)
            target = jnp.full((1, wide), -1, jnp.int32)
            for s in range(first, last):
                chip_s = owner(s)
                for m in (0, 1):
                    part = chip_s * 2 + (core if m == 0 else 1 - core)
                    start = (2 * (s - first) + m) * fp
                    inside = (lane >= start) & (lane < start + feat)
                    target = jnp.where(inside, lane - start + part * feat, target)
            source = lax.broadcasted_iota(jnp.int32, (rows.shape[1], wide), 0)
            mover = jnp.where(source == target, 1.0, 0.0).astype(jnp.bfloat16)
            out[pl.ds(k * rows_dev, rows_dev), :] = jnp.dot(
                rows, mover, preferred_element_type=jnp.float32).astype(jnp.bfloat16)

    def prepare_ids(k):
        base = doc * width
        ids = ids_all[k] - base
        ids = jnp.where((ids >= 0) & (ids < width), ids, -1)
        full = jnp.broadcast_to(ids, (128, rows_dev)).T
        lanes = lax.broadcasted_iota(jnp.int32, (rows_dev, 128), 1)
        idb[pl.ds(k * rows_dev, rows_dev), :] = jnp.where(full >= 0, full - lanes, -(2**20))

    full_tiles, rest = width // TILE, width % TILE

    def phase(index, from_tile, to_tile, with_rest):
        first, last = ranges[index]
        start, depth = 2 * first * fp, 2 * (last - first) * fp
        lhs = spread[index]

        def tile(col, wide):
            block = buf[pl.ds(start, depth), pl.ds(col, wide)]
            prod = jnp.dot(lhs[...], block, preferred_element_type=jnp.float32)
            w32 = block.astype(jnp.float32)
            sq = jnp.sum((w32 * w32).reshape(depth // 8, 8, wide), 0)
            if index == 0:
                acc[:, pl.ds(col, wide)] = prod
                csq[:, pl.ds(col, wide)] = sq
            else:
                acc[:, pl.ds(col, wide)] += prod
                csq[:, pl.ds(col, wide)] += sq

        @pl.loop(from_tile, to_tile)
        def _(t):
            tile(pl.multiple_of(t * TILE, TILE), TILE)

        if with_rest and rest:
            tile(full_tiles * TILE, rest)

    def final_rows(k, make_scale):
        first, last = ranges[2]
        start, depth = 2 * first * fp, 2 * (last - first) * fp
        rs = pl.ds(k * rows_dev, rows_dev)
        mx[rs, :] = jnp.full((rows_dev, 128), -3.0e38, jnp.float32)
        ch[rs, :] = jnp.zeros((rows_dev, 128), jnp.float32)

        def tile(col, wide):
            block = buf[pl.ds(start, depth), pl.ds(col, wide)]
            if make_scale:
                w32 = block.astype(jnp.float32)
                sq = jnp.sum((w32 * w32).reshape(depth // 8, 8, wide), 0) + csq[:, pl.ds(col, wide)]
                sc = lax.rsqrt(jnp.sum(sq, 0, keepdims=True) + epsilon)
                scale[:, pl.ds(col, wide)] = sc
            else:
                sc = scale[:, pl.ds(col, wide)]
            prod = jnp.dot(dp_c[rs, :], block, preferred_element_type=jnp.float32)
            v = (acc[rs, pl.ds(col, wide)] + prod) * sc
            for a in range(0, wide, 128):
                w = min(128, wide - a)
                va = v[:, a:a + w]
                mx[rs, pl.ds(0, w)] = jnp.maximum(mx[rs, pl.ds(0, w)], va)
                hit = idb[rs, pl.ds(0, w)] == col + a
                ch[rs, pl.ds(0, w)] = jnp.where(hit, va, ch[rs, pl.ds(0, w)])

        @pl.loop(0, full_tiles)
        def _(t):
            tile(pl.multiple_of(t * TILE, TILE), TILE)

        if rest:
            tile(full_tiles * TILE, rest)
        best = jnp.max(mx[rs, :].T, 0, keepdims=True)
        chosen = jnp.sum(ch[rs, :].T, 0, keepdims=True)
        return best, chosen

    permute(0)
    prepare_ids(0)
    wide = docs_all[0].astype(jnp.float32)
    squares = wide * wide
    total = squares[:, 0:128]
    for a in range(128, wide.shape[1], 128):
        total = total + squares[:, a:a + 128]
    scale_x = lax.rsqrt(jnp.sum(total.T, 0, keepdims=True) + epsilon)

    def step(way, h, c):
        s = slot(way, h)
        landed(s, 0, c)
        if h < reach(way, c):
            ring(way, h, c)
        share(s, c)

    half_tiles = full_tiles // 2
    for h in range(1, hops):
        last = h == hops - 1
        if last:
            for s in range(n - 3):
                for c in (0, 1):
                    landed(s, 1, c)
            phase(0, 0, half_tiles, False)
        step(0, h, 0)
        step(1, h, 1)
        if last:
            phase(0, half_tiles, full_tiles, True)
        step(0, h, 1)
        step(1, h, 0)
        if h == 1:
            for copy in doc_copies:
                copy.wait()
            for k in range(1, nd):
                permute(k)
                prepare_ids(k)
    for s in (n - 3, n - 2):
        for c in (0, 1):
            landed(s, 1, c)
    phase(1, 0, full_tiles, True)
    for way in (0, 1):
        landed(n - 1, 0, way)
        share(n - 1, way)
    for c in (0, 1):
        landed(n - 1, 1, c)

    returns = []
    for k in range(1, nd):
        best, chosen = final_rows(k, k == 1)
        res[k, 0:1, :] = best
        res[k, 1:2, :] = chosen
        copy = pltpu.make_async_remote_copy(
            src_ref=res.at[k], dst_ref=got.at[k], send_sem=res_send.at[k], recv_sem=res_recv.at[k],
            device_id={"doc": lax.rem(doc + nd - k, nd)}, device_id_type=MESH)
        copy.start()
        returns.append(copy)
    best, chosen = final_rows(0, nd == 1)
    for k in range(1, nd):
        returns[k - 1].wait()
        best = jnp.maximum(best, got[k, 0:1, :])
        chosen = chosen + got[k, 1:2, :]
    near_out[...] = 1.0 - best * scale_x
    chosen_out[...] = 1.0 - chosen * scale_x
    for copy in sent:
        copy.wait_send()


def on_device(docs, centroids, assigned):
    n_clu, nd = lax.axis_size("clu"), lax.axis_size("doc")
    n = n_clu // 2
    rows_dev, depth = docs.shape
    width, feat = centroids.shape
    fp = (feat + 15) // 16 * 16
    cents = centroids.T
    if fp != feat:
        cents = jnp.pad(cents, ((0, fp - feat), (0, 0)))
    rows = nd * rows_dev
    any_space = pl.BlockSpec(memory_space=pl.ANY)
    vmem = pl.BlockSpec(memory_space=pltpu.VMEM)
    dma = pltpu.SemaphoreType.DMA
    hops = n // 2
    line = jax.ShapeDtypeStruct((1, rows_dev), jnp.float32)
    near, chosen = pl.pallas_call(
        functools.partial(kernel, n, nd, feat),
        out_shape=(line, line),
        in_specs=[any_space] * 3,
        out_specs=(vmem, vmem),
        scratch_shapes=[
            pltpu.VMEM((n_clu * fp, width), jnp.bfloat16),
            pltpu.VMEM((nd, rows_dev, depth), jnp.bfloat16),
            pltpu.VMEM((nd, 1, rows_dev), jnp.int32),
            pltpu.VMEM((rows, (n - 3) * 2 * fp), jnp.bfloat16),
            pltpu.VMEM((rows, 4 * fp), jnp.bfloat16),
            pltpu.VMEM((rows, 2 * fp), jnp.bfloat16),
            pltpu.VMEM((rows, width), jnp.float32),
            pltpu.VMEM((rows, 128), jnp.int32),
            pltpu.VMEM((rows, 128), jnp.float32),
            pltpu.VMEM((rows, 128), jnp.float32),
            pltpu.VMEM((8, width), jnp.float32),
            pltpu.VMEM((1, width), jnp.float32),
            pltpu.VMEM((nd, 2, rows_dev), jnp.float32),
            pltpu.VMEM((nd, 2, rows_dev), jnp.float32),
            dma((3,)),
            dma((2, hops, 2)),
            dma((n, 2)),
            dma((n, 2, 2)),
            dma((nd,)), dma((nd,)), dma((nd,)), dma((nd,)), dma((nd,)), dma((nd,)),
        ],
        compiler_params=pltpu.CompilerParams(collective_id=0, has_side_effects=True),
        name="ring_distances",
    )(docs, cents, assigned.reshape(1, rows_dev))
    return near.reshape(rows_dev), chosen.reshape(rows_dev)


def solution(mesh):
    placed = (P(("clu", "doc"), None), P("doc", "clu"), P(("clu", "doc")))
    return jax.shard_map(
        on_device,
        mesh=mesh,
        in_specs=placed,
        out_specs=(P(("clu", "doc")), P(("clu", "doc"))),
        check_vma=False,
    )
```

time: 87.7 us -> 37.1 us (0.42)
  waiting for transfers between devices: 40.3 us -> 0 us
  Pallas kernels: 0 us -> 34.4 us
  blocking collectives: 25.1 us -> 0 us
  between operations: 14 us -> 0.65 us
  other arithmetic: 4.09 us -> 0 us
  matrix products: 3.71 us -> 0 us
  local copies, waits for them, and re-layouts: 0.25 us -> 1.86 us
    all_gather x1 -> x0, waiting for transfers between devices: 39.6 us -> none  [on_device(): block = lax.all_gather(centroids, 'clu', axis=1, tiled=True)]
    pallas_call x0 -> x1, Pallas kernels: none -> 34.4 us  [on_device(): pl.pallas_call(functools.partial(kernel, n, nd, feat), out_shape=(line, l...]
    all_gather x4 -> x0, blocking collectives: 25.1 us -> none  [the longest x1 10.8 us: on_device(): lax.all_gather(docs, 'doc', axis=0, tiled=True)]
    dot_general x1 -> x0, matrix products: 3.71 us -> none  [distances(): lax.dot_general(rows, cents, (((1,), (1,)), ((), ())), preferred_element_...]
    reduce_sum x2 -> x0, other arithmetic: 3.5 us -> none  [row_scales(): return lax.rsqrt(jnp.sum(wide * wide, 1) + epsilon)]
    unnamed x2 -> x6, local copies, waits for them, and re-layouts: 0.25 us -> 1.86 us
  transfers between devices with their start and end apart: 1 -> 0, of which waited for: 1 -> 0; matrix products, arithmetic and copies ran while one was open for 0% -> 0% of each run, Pallas kernels for 0% -> 0%
where the time goes in v1:
time: 37.1 us; the launch traced here: 36.9 us
  Pallas kernels  34.4 us (93%)
  local copies, waits for them, and re-layouts  1.86 us (5%)
  between operations  0.65 us (2%)
    pallas_call x1, Pallas kernels, on_device(): pl.pallas_call(functools.partial(kernel, n, nd, feat), out_shape=(line, l...  34.4 us
    unnamed x6, local copies, waits for them, and re-layouts  1.86 us

profile of v1, /device:TPU:0, one launch (start us, length us, event | category | flops | bytes accessed | tf_op | source)
XLA Modules:
  0.0 36.9 jit_solution(5867495838714718459)
XLA Ops:
  0.6 34.4 %ring_distances.1 = (f32[1,256]{1,0:T(1,128)}, f32[1,256]{1,0:T(1,128)}) custom-call(bf16[256,768]{1,0:T(8,128)(2,1)} %docs_in.1, bf16[48,2752]{1,0:T(8,128)(2,1)} %bitcast.4, s32[1,256]{1,0:T(1,128)} %bitcast.5), custom_call_target="tpu_custom_call" | custom-call | tf_op jit(solution)/shard_map/ring_distances/pallas_call | solution.py:291
  35.0 0.0 copy-start.1
  35.1 0.7 %copy-done.1 = f32[1,256]{1,0:T(1,128)S(1)} copy-done((f32[1,256]{1,0:T(1,128)S(1)}, f32[1,256]{1,0:T(1,128)}, u32[]{:S(2)}) %copy-start.1) | copy-done | bytes 1048
  35.7 0.0 copy-start
  35.7 0.6 %copy.7 = f32[256]{0:T(256)} copy(f32[256]{0:T(256)S(1)} %bitcast.7) | data formatting | bytes 2048
  36.3 0.1 copy-done
  36.3 0.6 %copy.8 = f32[256]{0:T(256)} copy(f32[256]{0:T(256)S(1)} %bitcast.6) | data formatting | bytes 2048
Async XLA Ops:
  35.0 0.7 %copy-start.1 = (f32[1,256]{1,0:T(1,128)S(1)}, f32[1,256]{1,0:T(1,128)}, u32[]{:S(2)}) copy-start(f32[1,256]{1,0:T(1,128)} %get-tuple-element.4) | copy-start | bytes 3076
  35.7 0.6 %copy-start = (f32[1,256]{1,0:T(1,128)S(1)}, f32[1,256]{1,0:T(1,128)}, u32[]{:S(2)}) copy-start(f32[1,256]{1,0:T(1,128)} %get-tuple-element.5) | copy-start | bytes 3076

commit v2 on v1

--- a/solution.py
+++ b/solution.py
@@ -8,13 +8,20 @@
 from jax.sharding import PartitionSpec as P
 
 epsilon = 1e-06
-TILE = 256
+PIECES = 4
+ROWS = 64
 MESH = pl.DeviceIdType.MESH
 
 
 def chip_at(pos, n):
     half = n // 2
     return jnp.where(pos < half, 2 * pos, 2 * (n - 1 - pos) + 1)
+
+
+def cut(width):
+    tiles = (width + 127) // 128
+    ends = [min(-(-tiles * (c + 1) // PIECES) * 128, width) for c in range(PIECES)]
+    return tuple((a, b - a) for a, b in zip([0] + ends[:-1], ends))
 
 
 def kernel(n, nd, feat, docs_in, cents_in, ids_in, near_out, chosen_out,
@@ -25,8 +32,8 @@
     fp = cents_in.shape[0]
     width = cents_in.shape[1]
     rows_dev = docs_in.shape[0]
-    cut = (width // 2 + 127) // 128 * 128
-    chunks = ((0, cut), (cut, width - cut))
+    chunks = cut(width)
+    half = len(chunks) // 2
 
     clu, doc = lax.axis_index("clu"), lax.axis_index("doc")
     core, chip = lax.rem(clu, 2), lax.div(clu, 2)
@@ -61,7 +68,7 @@
         return buf.at[pl.ds((2 * s + m) * fp, fp), pl.ds(*chunks[c])]
 
     def reach(way, c):
-        return hops if way == c else hops - 1
+        return hops if way == c // half else hops - 1
 
     sent = []
 
@@ -89,9 +96,10 @@
             device_id={"clu": partner}, device_id_type=MESH).wait_recv()
 
     own_c.wait()
-    for way, c in ((0, 0), (1, 1), (0, 1), (1, 0)):
-        ring(way, 0, c)
-    for c in (0, 1):
+    for i in range(PIECES):
+        ring(0, 0, i)
+        ring(1, 0, (i + half) % PIECES)
+    for c in range(PIECES):
         share(0, c)
     own_d.wait()
     own_i.wait()
@@ -145,67 +153,59 @@
         lanes = lax.broadcasted_iota(jnp.int32, (rows_dev, 128), 1)
         idb[pl.ds(k * rows_dev, rows_dev), :] = jnp.where(full >= 0, full - lanes, -(2**20))
 
-    full_tiles, rest = width // TILE, width % TILE
-
-    def phase(index, from_tile, to_tile, with_rest):
+    def phase(index, c):
         first, last = ranges[index]
         start, depth = 2 * first * fp, 2 * (last - first) * fp
-        lhs = spread[index]
-
-        def tile(col, wide):
-            block = buf[pl.ds(start, depth), pl.ds(col, wide)]
-            prod = jnp.dot(lhs[...], block, preferred_element_type=jnp.float32)
-            w32 = block.astype(jnp.float32)
-            sq = jnp.sum((w32 * w32).reshape(depth // 8, 8, wide), 0)
-            if index == 0:
-                acc[:, pl.ds(col, wide)] = prod
-                csq[:, pl.ds(col, wide)] = sq
-            else:
-                acc[:, pl.ds(col, wide)] += prod
-                csq[:, pl.ds(col, wide)] += sq
-
-        @pl.loop(from_tile, to_tile)
-        def _(t):
-            tile(pl.multiple_of(t * TILE, TILE), TILE)
-
-        if with_rest and rest:
-            tile(full_tiles * TILE, rest)
-
-    def final_rows(k, make_scale):
-        first, last = ranges[2]
-        start, depth = 2 * first * fp, 2 * (last - first) * fp
-        rs = pl.ds(k * rows_dev, rows_dev)
-        mx[rs, :] = jnp.full((rows_dev, 128), -3.0e38, jnp.float32)
-        ch[rs, :] = jnp.zeros((rows_dev, 128), jnp.float32)
-
-        def tile(col, wide):
-            block = buf[pl.ds(start, depth), pl.ds(col, wide)]
-            if make_scale:
-                w32 = block.astype(jnp.float32)
-                sq = jnp.sum((w32 * w32).reshape(depth // 8, 8, wide), 0) + csq[:, pl.ds(col, wide)]
-                sc = lax.rsqrt(jnp.sum(sq, 0, keepdims=True) + epsilon)
-                scale[:, pl.ds(col, wide)] = sc
-            else:
-                sc = scale[:, pl.ds(col, wide)]
-            prod = jnp.dot(dp_c[rs, :], block, preferred_element_type=jnp.float32)
-            v = (acc[rs, pl.ds(col, wide)] + prod) * sc
+        cols = pl.ds(*chunks[c])
+        block = buf[pl.ds(start, depth), cols]
+        prod = jnp.dot(spread[index][...], block, preferred_element_type=jnp.float32)
+        w32 = block.astype(jnp.float32)
+        sq = jnp.sum((w32 * w32).reshape(depth // 8, 8, chunks[c][1]), 0)
+        if index == 0:
+            acc[:, cols] = prod
+            csq[:, cols] = sq
+        else:
+            acc[:, cols] += prod
+            csq[:, cols] += sq
+
+    tail = pl.ds(2 * (n - 1) * fp, 2 * fp)
+
+    def finish_scale(c):
+        cols = pl.ds(*chunks[c])
+        w32 = buf[tail, cols].astype(jnp.float32)
+        sq = jnp.sum((w32 * w32).reshape(2 * fp // 8, 8, chunks[c][1]), 0) + csq[:, cols]
+        scale[:, cols] = lax.rsqrt(jnp.sum(sq, 0, keepdims=True) + epsilon)
+
+    def final(k, c):
+        start, wide = chunks[c]
+        prod = jnp.dot(dp_c[pl.ds(k * rows_dev, rows_dev), :], buf[tail, pl.ds(start, wide)],
+                       preferred_element_type=jnp.float32)
+        for r in range(0, rows_dev, ROWS):
+            rs = pl.ds(k * rows_dev + r, ROWS)
+            top, hit = mx[rs, :], ch[rs, :]
+            ids = idb[rs, :]
             for a in range(0, wide, 128):
                 w = min(128, wide - a)
-                va = v[:, a:a + w]
-                mx[rs, pl.ds(0, w)] = jnp.maximum(mx[rs, pl.ds(0, w)], va)
-                hit = idb[rs, pl.ds(0, w)] == col + a
-                ch[rs, pl.ds(0, w)] = jnp.where(hit, va, ch[rs, pl.ds(0, w)])
-
-        @pl.loop(0, full_tiles)
-        def _(t):
-            tile(pl.multiple_of(t * TILE, TILE), TILE)
-
-        if rest:
-            tile(full_tiles * TILE, rest)
-        best = jnp.max(mx[rs, :].T, 0, keepdims=True)
-        chosen = jnp.sum(ch[rs, :].T, 0, keepdims=True)
-        return best, chosen
-
+                cols = pl.ds(start + a, w)
+                v = (acc[rs, cols] + prod[r:r + ROWS, a:a + w]) * scale[:, cols]
+                if w == 128:
+                    top = jnp.maximum(top, v)
+                    hit = jnp.where(ids == start + a, v, hit)
+                else:
+                    mx[rs, :] = top
+                    ch[rs, :] = hit
+                    mx[rs, pl.ds(0, w)] = jnp.maximum(mx[rs, pl.ds(0, w)], v)
+                    ch[rs, pl.ds(0, w)] = jnp.where(idb[rs, pl.ds(0, w)] == start + a, v, ch[rs, pl.ds(0, w)])
+            if wide % 128 == 0:
+                mx[rs, :] = top
+                ch[rs, :] = hit
+
+    def reduced(k):
+        rs = pl.ds(k * rows_dev, rows_dev)
+        return (jnp.max(mx[rs, :].T, 0, keepdims=True), jnp.sum(ch[rs, :].T, 0, keepdims=True))
+
+    mx[...] = jnp.full(mx.shape, -3.0e38, jnp.float32)
+    ch[...] = jnp.zeros(ch.shape, jnp.float32)
     permute(0)
     prepare_ids(0)
     wide = docs_all[0].astype(jnp.float32)
@@ -222,39 +222,54 @@
             ring(way, h, c)
         share(s, c)
 
-    half_tiles = full_tiles // 2
+    def pair(h, i):
+        step(0, h, i)
+        step(1, h, (i + half) % PIECES)
+
+    def partners(slots, c):
+        for s in slots:
+            landed(s, 1, c)
+
+    early, late = range(n - 3), (n - 3, n - 2)
+    order = [j // 2 + half * (j % 2) for j in range(PIECES)]
     for h in range(1, hops):
-        last = h == hops - 1
-        if last:
-            for s in range(n - 3):
-                for c in (0, 1):
-                    landed(s, 1, c)
-            phase(0, 0, half_tiles, False)
-        step(0, h, 0)
-        step(1, h, 1)
-        if last:
-            phase(0, half_tiles, full_tiles, True)
-        step(0, h, 1)
-        step(1, h, 0)
-        if h == 1:
-            for copy in doc_copies:
-                copy.wait()
-            for k in range(1, nd):
-                permute(k)
-                prepare_ids(k)
-    for s in (n - 3, n - 2):
-        for c in (0, 1):
-            landed(s, 1, c)
-    phase(1, 0, full_tiles, True)
-    for way in (0, 1):
-        landed(n - 1, 0, way)
-        share(n - 1, way)
-    for c in (0, 1):
+        for i in range(PIECES):
+            pair(h, i)
+            if h == hops - 2 and i == half:
+                for copy in doc_copies:
+                    copy.wait()
+                for k in range(1, nd):
+                    permute(k)
+                    prepare_ids(k)
+            if h == hops - 1:
+                c = order[i]
+                partners(early, c)
+                phase(0, c)
+    for c in order[:half]:
+        partners(late, c)
+        phase(1, c)
+    for i in range(half):
+        for way in (0, 1):
+            c = i + half * way
+            landed(n - 1, 0, c)
+            share(n - 1, c)
+    for c in order[half:]:
+        partners(late, c)
+        phase(1, c)
+    for c in order[:-2]:
         landed(n - 1, 1, c)
+        finish_scale(c)
+        for k in range(nd):
+            final(k, c)
+    for c in order[-2:]:
+        landed(n - 1, 1, c)
+        finish_scale(c)
 
     returns = []
     for k in range(1, nd):
-        best, chosen = final_rows(k, k == 1)
+        for c in order[-2:]:
+            final(k, c)
+        best, chosen = reduced(k)
         res[k, 0:1, :] = best
         res[k, 1:2, :] = chosen
         copy = pltpu.make_async_remote_copy(
@@ -262,13 +277,15 @@
             device_id={"doc": lax.rem(doc + nd - k, nd)}, device_id_type=MESH)
         copy.start()
         returns.append(copy)
-    best, chosen = final_rows(0, nd == 1)
+    for c in order[-2:]:
+        final(0, c)
+    best, chosen = reduced(0)
     for k in range(1, nd):
         returns[k - 1].wait()
         best = jnp.maximum(best, got[k, 0:1, :])
         chosen = chosen + got[k, 1:2, :]
-    near_out[...] = 1.0 - best * scale_x
-    chosen_out[...] = 1.0 - chosen * scale_x
+    near_out[...] = best * scale_x
+    chosen_out[...] = chosen * scale_x
     for copy in sent:
         copy.wait_send()
 
@@ -309,15 +326,15 @@
             pltpu.VMEM((nd, 2, rows_dev), jnp.float32),
             pltpu.VMEM((nd, 2, rows_dev), jnp.float32),
             dma((3,)),
-            dma((2, hops, 2)),
-            dma((n, 2)),
-            dma((n, 2, 2)),
+            dma((2, hops, PIECES)),
+            dma((n, PIECES)),
+            dma((n, 2, PIECES)),
             dma((nd,)), dma((nd,)), dma((nd,)), dma((nd,)), dma((nd,)), dma((nd,)),
         ],
         compiler_params=pltpu.CompilerParams(collective_id=0, has_side_effects=True),
         name="ring_distances",
     )(docs, cents, assigned.reshape(1, rows_dev))
-    return near.reshape(rows_dev), chosen.reshape(rows_dev)
+    return 1.0 - near.reshape(rows_dev), 1.0 - chosen.reshape(rows_dev)
 
 
 def solution(mesh):

time: 37.1 us -> 34.6 us (0.933)
  Pallas kernels: 34.4 us -> 32.6 us
  local copies, waits for them, and re-layouts: 1.86 us -> 0.63 us
  other arithmetic: 0 us -> 0.57 us
    pallas_call x1, Pallas kernels: 34.4 us -> 32.6 us  [on_device(): pl.pallas_call(functools.partial(kernel, n, nd, feat), out_shape=(line, l...]
    unnamed x6 -> x4, local copies, waits for them, and re-layouts: 1.86 us -> 0.63 us
    sub x0 -> x1, other arithmetic: none -> 0.57 us  [on_device(): return (1.0 - near.reshape(rows_dev), 1.0 - chosen.reshape(rows_dev))]
where the time goes in v2:
time: 34.6 us; the launch traced here: 34.5 us
  Pallas kernels  32.6 us (94%)
  between operations  0.65 us (2%)
  local copies, waits for them, and re-layouts  0.63 us (2%)
  other arithmetic  0.57 us (2%)
    pallas_call x1, Pallas kernels, on_device(): pl.pallas_call(functools.partial(kernel, n, nd, feat), out_shape=(line, l...  32.6 us

profile of v2, /device:TPU:0, one launch (start us, length us, event | category | flops | bytes accessed | tf_op | source)
XLA Modules:
  0.0 34.5 jit_solution(5199725418724960359)
XLA Ops:
  0.6 32.6 %ring_distances.1 = (f32[1,256]{1,0:T(1,128)}, f32[1,256]{1,0:T(1,128)}) custom-call(bf16[256,768]{1,0:T(8,128)(2,1)} %docs_in.1, bf16[48,2752]{1,0:T(8,128)(2,1)} %bitcast.4, s32[1,256]{1,0:T(1,128)} %bitcast.5), custom_call_target="tpu_custom_call" | custom-call | tf_op jit(solution)/shard_map/ring_distances/pallas_call | solution.py:308
  33.2 0.0 copy-start.1
  33.3 0.0 copy-start
  33.3 0.6 %copy-done.1 = f32[1,256]{1,0:T(1,128)S(1)} copy-done((f32[1,256]{1,0:T(1,128)S(1)}, f32[1,256]{1,0:T(1,128)}, u32[]{:S(2)}) %copy-start.1) | copy-done | bytes 1048
  33.9 0.0 copy-done
  33.9 0.6 %broadcast_subtract_fusion = (f32[1,256]{1,0:T(1,128)}, f32[1,256]{1,0:T(1,128)}) fusion(f32[1,256]{1,0:T(1,128)S(1)} %copy-done.1, f32[1,256]{1,0:T(1,128)S(1)} %copy-done), kind=kLoop, calls=%fused_computation | loop fusion | flops 512 | bytes 4096 | tf_op jit(solution)/shard_map/sub | solution.py:337
Async XLA Ops:
  33.2 0.6 %copy-start.1 = (f32[1,256]{1,0:T(1,128)S(1)}, f32[1,256]{1,0:T(1,128)}, u32[]{:S(2)}) copy-start(f32[1,256]{1,0:T(1,128)} %get-tuple-element.5) | copy-start | bytes 3076
  33.3 0.6 %copy-start = (f32[1,256]{1,0:T(1,128)S(1)}, f32[1,256]{1,0:T(1,128)}, u32[]{:S(2)}) copy-start(f32[1,256]{1,0:T(1,128)} %get-tuple-element.4) | copy-start | bytes 3076
